TPU v7x, 768 devices: a whole 4x8x12 slice. The times are simulated.
768 devices in a mesh: section: 32 (over y, z_lo), fsdp: 24 (over x, z_hi, core).
Axes of the slice: x: 4, y: 8, z: 12 (z_hi: 3, z_lo: 4; z = z_hi * 4 + z_lo), core: 2. Of those that a mesh axis runs over, the one named last changes fastest.
Arguments:
- source_rows: bfloat16 [12288, 4096], P(('section', 'fsdp')), may hold values from -6 to 6
- target_rows: bfloat16 [4096, 4096], P('section'), may hold values from -6 to 6
- attn_weights: bfloat16 [32, 4, 4096, 3072], P('section', None, None, 'fsdp'), may hold values from -3.76875 to 3.76875
- gains: float32 [32, 4096], P('section'), may hold values from 0.25 to 1.75
- lengths: int32 [32], P('section'), may hold values from 192 to 384
Outputs:
- source_next: bfloat16 [12288, 4096], P(('section', 'fsdp'))
- target_next: bfloat16 [4096, 4096], P('section')
Inputs may be any that keep to these rules, and one draw needn't show every extreme that they name: Keys at positions lengths[s] and beyond are padding.
All inputs are finite; a program needn't handle non-finite values.
Results may differ from a plain program's by a relative error of at most 0.015.
The roundings to bfloat16 on the way count: a program that leaves them out, or rounds other values in their place, can miss the bound.
Values may be sent and summed in bfloat16 or wider, within the bound.
A program may use at most 64 MiB of HBM per device.

v0:
```python
import jax
import jax.numpy as jnp
from jax import lax
from jax.sharding import PartitionSpec as P

HEAD_DIM = 64


def from_everyone(value, axis):
    copies = jnp.broadcast_to(value, (lax.axis_size(axis), *value.shape))
    return lax.all_to_all(copies, axis, split_axis=0, concat_axis=0, tiled=True)


def laid_out(pieces, dim):
    pieces = jnp.moveaxis(pieces, 0, dim)
    lengths = pieces.shape
    return pieces.reshape(*lengths[:dim], lengths[dim] * lengths[dim + 1], *lengths[dim + 2 :])


def collect(value, axis, dim):
    pieces = from_everyone(value, axis)
    return laid_out(pieces, dim)


def shifted(value, axis, steps):
    count = lax.axis_size(axis)
    pairs = [(source, (source + steps) % count) for source in range(count)]
    return lax.ppermute(value, axis, pairs)


def rms_norm(block_rows, gain_row):
    widened = block_rows.astype(jnp.float32)
    inverse_rms = lax.rsqrt(jnp.mean(widened * widened, axis=-1, keepdims=True) + 1e-06)
    return (widened * inverse_rms * gain_row).astype(jnp.bfloat16)


def project(block_rows, weight):
    return jnp.dot(block_rows, weight, preferred_element_type=jnp.float32).astype(jnp.bfloat16)


def attend(queries, key_rows, values, length):
    query_count = queries.shape[0]
    key_count = key_rows.shape[0]
    head_count = queries.shape[1] // HEAD_DIM
    query_heads = queries.reshape(query_count, head_count, HEAD_DIM)
    key_heads = key_rows.reshape(key_count, head_count, HEAD_DIM)
    value_heads = values.reshape(key_count, head_count, HEAD_DIM)
    scores = (
        jnp.einsum("qhc,khc->hqk", query_heads, key_heads, preferred_element_type=jnp.float32)
        * 0.125
    )
    key_valid = jnp.arange(key_count, dtype=jnp.int32) < length
    scores = jnp.where(key_valid[None, None, :], scores, -1000000000.0)
    row_max = jnp.max(scores, axis=-1, keepdims=True)
    expo = jnp.exp(scores - row_max)
    soft = (expo / jnp.sum(expo, axis=-1, keepdims=True)).astype(jnp.bfloat16)
    context = jnp.einsum("hqk,khc->qhc", soft, value_heads, preferred_element_type=jnp.float32)
    return context.reshape(query_count, head_count * HEAD_DIM).astype(jnp.bfloat16)


def out_partial(context, out_weight):
    return lax.dot_general(
        context, out_weight, (((1,), (1,)), ((), ())), preferred_element_type=jnp.float32
    )


def pad_rows(block, total_rows):
    return jnp.pad(block, ((0, 0), (0, total_rows - block.shape[1]), (0, 0)))


def local(source_rows, target_rows, attn_weights, gains, lengths):
    section_index = lax.axis_index("section")
    encoder_section = section_index < lax.axis_size("section") // 2
    group_count = lax.axis_size("fsdp")
    weights = attn_weights[0]
    gain_row = gains[0]
    length = lengths[0]
    source_whole = lax.all_gather(source_rows, "fsdp", axis=0, tiled=True)

    def encoder_work(whole_rows, target_block):
        normed = rms_norm(whole_rows, gain_row)
        context = attend(
            project(normed, weights[0]),
            project(normed, weights[1]),
            project(normed, weights[2]),
            length,
        )
        return (out_partial(context, weights[3]), jnp.zeros(target_block.shape, jnp.float32))

    def decoder_work(whole_rows, target_block):
        normed = rms_norm(target_block, gain_row)
        context = attend(
            project(normed, weights[0]),
            project(whole_rows, weights[1]),
            project(whole_rows, weights[2]),
            length,
        )
        return (jnp.zeros(whole_rows.shape, jnp.float32), out_partial(context, weights[3]))

    source_terms, target_terms = lax.cond(
        encoder_section, encoder_work, decoder_work, source_whole, target_rows
    )
    own_rows = source_rows.shape[0]
    target_count = target_rows.shape[0]
    width = target_rows.shape[1]
    share_rows = (target_count + group_count - 1) // group_count
    slot_rows = max(own_rows, share_rows)
    target_padded = jnp.pad(target_terms, ((0, share_rows * group_count - target_count), (0, 0)))
    source_slots = pad_rows(source_terms.reshape(group_count, own_rows, width), slot_rows)
    target_slots = pad_rows(target_padded.reshape(group_count, share_rows, width), slot_rows)
    slot_sum = lax.psum_scatter(
        (source_slots + target_slots).astype(jnp.bfloat16), "fsdp", scatter_dimension=0, tiled=True
    ).astype(jnp.float32)[0]
    source_sum = jnp.where(encoder_section, slot_sum, 0.0)
    source_new = (source_rows.astype(jnp.float32) + source_sum).astype(jnp.bfloat16)
    target_share_sum = jnp.where(encoder_section, 0.0, slot_sum[:share_rows])
    rows_padded = jnp.pad(target_rows, ((0, share_rows * group_count - target_count), (0, 0)))
    group_index = lax.axis_index("fsdp")
    own_targets = lax.dynamic_slice_in_dim(rows_padded, group_index * share_rows, share_rows, 0)
    share_new = (own_targets.astype(jnp.float32) + target_share_sum).astype(jnp.bfloat16)
    gathered = collect(share_new, "fsdp", 0)
    target_new = gathered[:target_count]
    source_next, target_next = shifted((source_new, target_new), "section", 1)
    return (source_next, target_next)


def solution(mesh):
    in_specs = (
        P(("section", "fsdp"), None),
        P("section", None),
        P("section", None, None, "fsdp"),
        P("section", None),
        P("section"),
    )
    out_specs = (P(("section", "fsdp"), None), P("section", None))
    return jax.shard_map(local, mesh=mesh, in_specs=in_specs, out_specs=out_specs, check_vma=False)
```

profile of v0, /device:TPU:1, one launch (start us, length us, event | category | flops | bytes accessed | tf_op | source)
XLA Modules:
  0.0 377.2 jit_solution(16145491004800631078)
XLA Ops:
  7.2 0.0 all-gather.2.cloned.1.call-start
  7.2 0.7 all-gather.2.cloned.1.call-update
  7.9 0.0 reduce-scatter.2.cloned.1.call-start
  8.0 95.5 %all-gather.2.cloned.1.call-done = bf16[384,4096]{1,0:T(8,128)(2,1)} async-done(((bf16[16,4096]{1,0:T(8,128)(2,1)}), bf16[384,4096]{1,0:T(8,128)(2,1)}) %all-gather.2.cloned.1.call-update) | async-done | bytes 3145744 | tf_op jit(solution)/shard_map/all_gather | solution.py:78
  103.4 19.6 %conditional.1 = (f32[24,16,4096]{2,1,0:T(8,128)}, f32[24,16,4096]{2,1,0:T(8,128)}) conditional(s32[]{:T(128)} %convert_element_type.80, (bf16[4,4096,128]{2,1,0:T(8,128)(2,1)}, bf16[384,4096]{1,0:T(8,128)(2,1)}, s32[]{:T(128)}, bf16[128,4096]{1,0:T(8,128)(2,1)}, f32[1,4096]{1,0:T(1,128)}) %tuple.31, (bf16[384,4096]{1,0:T(8,128)(2,1)}, ...), branch_computations={%region_0.4_spmd, %region_4.8_spmd} | conditional | flops 1737722112 | bytes 71205360 | solution.py:100
  103.4 0.0 copy-start.1
  103.4 0.0 copy-start.6
  103.4 0.8 iota_compare_fusion.1
  104.3 2.7 fusion.23
  107.0 0.0 copy-done.1
  107.0 0.0 copy-done.6
  107.0 1.2 fusion.25
  108.2 0.1 pad.20
  108.3 0.0 copy-start.2
  108.3 2.4 convolution_convert_fusion.5
  110.7 0.1 copy-done.2
  110.8 1.0 convolution_convert_fusion.6
  111.8 1.0 convolution_convert_fusion.7
  112.9 0.6 fusion.52
  113.4 0.8 fusion.29
  114.2 0.2 copy.10
  114.4 0.1 dot_general.36
  114.5 0.3 pad.21
  114.8 3.4 pad.22
  118.1 4.9 %fusion.30 = f32[24,16,4096]{2,1,0:T(8,128)} fusion(bf16[24,16,128]{2,1,0:T(8,128)(2,1)S(1)} %dot_general.36, bf16[4,4096,128]{2,1,0:T(8,128)(2,1)} %get-tuple-element.27), kind=kOutput, calls=%fused_computation.47 | convolution fusion | flops 402653184 | bytes 7438336 | tf_op jit(solution)/shard_map/cond/branch_1_fun/dot_general | solution.py:62
  123.0 7.1 %add_convert_fusion = bf16[24,16,4096]{2,1,0:T(8,128)(2,1)} fusion(f32[24,16,4096]{2,1,0:T(8,128)} %get-tuple-element.33, f32[24,16,4096]{2,1,0:T(8,128)} %get-tuple-element.34), kind=kLoop, calls=%fused_computation.64 | loop fusion | flops 3145728 | bytes 15728640 | tf_op jit(solution)/shard_map/convert_element_type | solution.py:112
  130.1 0.0 copy-start.3
  130.1 0.0 reduce-scatter.2.cloned.1.call-update
  130.2 142.6 %reduce-scatter.2.cloned.1.call-done = bf16[1,16,4096]{2,1,0:T(8,128)(2,1)} async-done(((bf16[24,16,4096]{2,1,0:T(8,128)(2,1)}), bf16[1,16,4096]{2,1,0:T(8,128)(2,1)}) %reduce-scatter.2.cloned.1.call-update) | async-done | bytes 131088 | tf_op jit(solution)/shard_map/reduce_scatter | solution.py:111
  272.7 0.9 convert_element_type.82
  273.7 0.0 copy-done.3
  273.7 0.1 fusion.50
  273.7 0.2 broadcast_in_dim.45
  273.9 62.2 %all_to_all.5 = bf16[24,6,4096]{2,1,0:T(8,128)(2,1)S(1)} all-to-all(bf16[24,6,4096]{2,1,0:T(8,128)(2,1)S(1)} %broadcast_in_dim.45), channel_id=1, replica_groups=mesh['section'=32,'fsdp'=24] {'fsdp'}, dimensions={0} | all-to-all | bytes 2359296 | tf_op jit(solution)/shard_map/all_to_all | solution.py:11
  336.1 0.0 copy-start.4
  336.1 0.0 copy-start.5
  336.1 0.4 reshape.80
  336.5 0.1 slice.34
  336.6 1.9 collective-permute-start.1
  338.5 0.0 copy-done.4
  338.5 0.0 copy-done.5
  338.6 1.9 collective-permute-start
  340.5 28.2 %collective-permute-done = bf16[16,4096]{1,0:T(8,128)(2,1)S(1)} collective-permute-done((bf16[16,4096]{1,0:T(8,128)(2,1)S(1)}, bf16[16,4096]{1,0:T(8,128)(2,1)S(1)}, u32[]{:S(2)}, u32[]{:S(2)}) %collective-permute-start) | collective-permute-done | bytes 131104 | tf_op jit(solution)/shard_map/ppermute | solution.py:28
  368.7 0.0 collective-permute-done.1
  368.7 0.7 copy.18
  369.4 1.0 copy.19
  (4 shorter events, 0.1 us)
Async XLA Ops:
  7.2 96.3 %all-gather.2.cloned.1.call-start = ((), (), s32[]{:S(2)}) async-start(), calls=%async_computation.2 | async-start | bytes 3276800 | tf_op jit(solution)/shard_map/all_gather | solution.py:78
  7.9 264.8 %reduce-scatter.2.cloned.1.call-start = ((), (), s32[]{:S(2)}) async-start(), calls=%async_computation.3 | async-start | bytes 3276800 | tf_op jit(solution)/shard_map/reduce_scatter | solution.py:111
  103.4 3.6 copy-start.1
  103.4 3.6 copy-start.6
  108.3 2.5 copy-start.2
  130.1 143.6 %copy-start.3 = (bf16[128,4096]{1,0:T(8,128)(2,1)S(1)}, bf16[128,4096]{1,0:T(8,128)(2,1)}, u32[]{:S(2)}) copy-start(bf16[128,4096]{1,0:T(8,128)(2,1)} %param.8) | copy-start | bytes 3145732
  336.1 2.5 copy-start.4
  336.1 2.5 copy-start.5
  336.6 32.1 %collective-permute-start.1 = (bf16[128,4096]{1,0:T(8,128)(2,1)S(1)}, bf16[128,4096]{1,0:T(8,128)(2,1)S(1)}, u32[]{:S(2)}, u32[]{:S(2)}) collective-permute-start(bf16[128,4096]{1,0:T(8,128)(2,1)S(1)} %slice.34), channel_id=1, source_target_pairs={{0,24},{24,48},{48,72},{72,96},{96,120},{120,144},{144,168},{168,1... | collective-permute-start | bytes 3145736 | tf_op jit(solution)/shard_map/ppermute | solution.py:28
  338.6 30.1 %collective-permute-start = (bf16[16,4096]{1,0:T(8,128)(2,1)S(1)}, bf16[16,4096]{1,0:T(8,128)(2,1)S(1)}, u32[]{:S(2)}, u32[]{:S(2)}) collective-permute-start(bf16[16,4096]{1,0:T(8,128)(2,1)S(1)} %fusion.47), channel_id=1, source_target_pairs={{0,24},{24,48},{48,72},{72,96},{96,120},{120,144},{144,168},{168,1... | collective-permute-start | bytes 393224 | tf_op jit(solution)/shard_map/ppermute | solution.py:28
Sparse Core Ops, SparseCore 0:
  12.0 91.3 all-gather.1
  130.3 142.4 reduce-scatter.1
where the time goes:
time: 378 us; the launch traced here: 377 us
  waiting for transfers between devices  267 us (71%)
  blocking collectives  62.2 us (16%)
  between operations  14.1 us (4%)
  other arithmetic  12.8 us (3%)
  matrix products  10.6 us (3%)
  local copies, waits for them, and re-layouts  6.46 us (2%)
  starting transfers between devices  3.92 us (1%)
    reduce_scatter x1, waiting for transfers between devices, local(): lax.psum_scatter((source_slots + target_slots).astype(jnp.bfloat16), 'fsd...  143 us
    all_gather x1, waiting for transfers between devices, local(): source_whole = lax.all_gather(source_rows, 'fsdp', axis=0, tiled=True)  95.5 us
    all_to_all x1, blocking collectives, from_everyone(): return lax.all_to_all(copies, axis, split_axis=0, concat_axis=0, tiled=True)  62.2 us
    ppermute x2, waiting for transfers between devices, shifted(): return lax.ppermute(value, axis, pairs)  28.2 us
  transfers between devices with their start and end apart: 4, of which 3 were waited for; matrix products, arithmetic and copies ran while one was open for 0% of the time, Pallas kernels for 0%

commit v1 on v0

v1 whole, which is shorter than its diff:
```python
import functools

import jax
import jax.numpy as jnp
from jax import lax
from jax.experimental import pallas as pl
from jax.experimental.pallas import tpu as pltpu
from jax.sharding import PartitionSpec as P

HEAD_DIM = 64
NX = 4
NZ = 3
NCORE = 2
CHUNKS = 4
MESH = pl.DeviceIdType.MESH


def kernel(
    sections,
    x_hbm,
    y_hbm,
    w_hbm,
    g_hbm,
    len_ref,
    xout,
    yout,
    xin,
    yin,
    gain,
    wqkv,
    wout,
    rows,
    normy,
    accq,
    acckv,
    kv,
    ctx,
    terms,
    r1,
    r2,
    zs,
    part,
    fin,
    ld,
    w_s,
    w_r,
    ag_s,
    az,
    ax,
    af,
    kv_s,
    kv_r,
    e_s,
    e_r,
    rs_s,
    c1,
    c2,
    c3,
    l_s,
    l_r,
    y_s,
    yx,
    yf,
    yp,
):
    own, width = xin.shape
    targets = yin.shape[0]
    lanes = w_hbm.shape[2]
    W = width // CHUNKS
    H = W // 2
    plane = NX * NZ * own
    tplane = NX * own

    s = lax.axis_index("section")
    f = lax.axis_index("fsdp")
    c = lax.rem(f, NCORE)
    zh = lax.rem(f // NCORE, NZ)
    x = f // (NCORE * NZ)
    xr, xl, x2 = lax.rem(x + 1, NX), lax.rem(x + 3, NX), lax.rem(x + 2, NX)
    zu, zd = lax.rem(zh + 1, NZ), lax.rem(zh + 2, NZ)
    s_next, s_prev = lax.rem(s + 1, sections), lax.rem(s + sections - 1, sections)
    enc = s < sections // 2
    dec = jnp.logical_not(enc)
    src_enc = s_prev < sections // 2
    src_dec = jnp.logical_not(src_enc)

    def fid(px, pz, pc):
        return {"fsdp": (px * NZ + pz) * NCORE + pc}

    right, left = fid(xr, zh, c), fid(xl, zh, c)
    up, down = fid(x, zu, c), fid(x, zd, c)
    partner = fid(x, zh, 1 - c)
    forward, backward = {"section": s_next}, {"section": s_prev}
    xdev, xnb = (right, left), (xr, xl)

    def rdma(src, dst, send, recv, dev):
        return pltpu.make_async_remote_copy(
            src_ref=src, dst_ref=dst, send_sem=send, recv_sem=recv, device_id=dev, device_id_type=MESH
        )

    def cols(j):
        return pl.ds(pl.multiple_of(j * W, W), W)

    def half(j, d):
        return pl.ds(pl.multiple_of(j * W + d * H, H), H)

    def blk(k):
        return pl.ds(pl.multiple_of(k * own, own), own)

    ld_x = pltpu.make_async_copy(x_hbm, xin, ld.at[0])
    ld_g = pltpu.make_async_copy(g_hbm, gain, ld.at[1])
    ld_y = pltpu.make_async_copy(y_hbm, yin, ld.at[2])
    ld_x.start()
    ld_g.start()
    ld_y.start()

    barrier = pltpu.get_barrier_semaphore()
    for dev in (partner, right, left, up, down, forward, backward):
        pl.semaphore_signal(barrier, inc=1, device_id=dev, device_id_type=MESH)

    def wslot(i):
        if i < 3:
            return wqkv.at[:, pl.ds(pl.multiple_of(i * NCORE * lanes + c * lanes, lanes), lanes)]
        return wout.at[c]

    ld_w = [pltpu.make_async_copy(w_hbm.at[i], wslot(i), ld.at[3 + i]) for i in range(4)]
    for copy in ld_w:
        copy.start()

    k_own = x * NZ + zh
    ld_x.wait()
    ld_g.wait()

    def normed(block):
        wide = block.astype(jnp.float32)
        inv = lax.rsqrt(jnp.mean(wide * wide, axis=-1, keepdims=True) + 1e-06)
        return (wide * inv * gain[...]).astype(jnp.bfloat16)

    @pl.when(enc)
    def _():
        rows[blk(k_own), :] = normed(xin[...])

    @pl.when(dec)
    def _():
        rows[blk(k_own), :] = xin[...]

    pl.semaphore_wait(barrier, 7)

    zdev = (up, down)
    zb = (zh, zd, zu)
    zfrom = (zd, zu)

    def az_copy(u, j, k):
        ref = rows.at[blk(k), cols(j)]
        return rdma(ref, ref, ag_s, az.at[u, j], zdev[u])

    def ax_copy(b, d, j, k):
        ref = rows.at[blk(k), cols(j)]
        return rdma(ref, ref, ag_s, ax.at[b, d, j], xdev[d])

    def af_copy(b, d, j, k):
        ref = rows.at[blk(k), half(j, d)]
        return rdma(ref, ref, ag_s, af.at[b, d, j], xdev[d])

    @pl.loop(0, CHUNKS)
    def _(j):
        for u in range(2):
            az_copy(u, j, k_own).start()
        for d in range(2):
            ax_copy(0, d, j, k_own).start()

    push_w = [rdma(w_hbm.at[i], wslot(i), w_s, w_r.at[i], partner) for i in range(4)]
    for copy in push_w:
        copy.start()

    ld_y.wait()

    @pl.when(dec)
    def _():
        @pl.loop(0, NX)
        def _(i):
            normy[blk(i), :] = normed(yin[blk(i * NCORE + c), :])

    def relay(b, j):
        for d, origin in ((0, xl), (1, xr)):
            k = origin * NZ + zb[b]
            ax_copy(b, d, j, k).wait_recv()
            af_copy(b, d, j, k).start()

    @pl.loop(0, CHUNKS)
    def _(j):
        relay(0, j)

    accq[...] = jnp.zeros_like(accq)
    acckv[...] = jnp.zeros_like(acckv)
    qw = NCORE * lanes

    @pl.loop(0, CHUNKS + 1)
    def _(j):
        @pl.when(j < CHUNKS)
        def _():
            for u in range(2):
                k = x * NZ + zfrom[u]
                az_copy(u, j, k).wait_recv()
                for d in range(2):
                    ax_copy(1 + u, d, j, k).start()
            for b in (1, 2):
                relay(b, j)

        @pl.when(j == 0)
        def _():
            for i in range(3):
                ld_w[i].wait()
                push_w[i].wait_recv()

        @pl.when(j > 0)
        def _():
            jj = j - 1
            for b in range(3):
                for d in range(2):
                    af_copy(b, d, jj, x2 * NZ + zb[b]).wait_recv()
            wc = wqkv.at[cols(jj), :]
            acckv[...] += jnp.dot(rows[:, cols(jj)], wc[:, qw:], preferred_element_type=jnp.float32)

            @pl.when(enc)
            def _():
                accq[...] += jnp.dot(rows[:, cols(jj)], wc[:, :qw], preferred_element_type=jnp.float32)

            @pl.when(dec)
            def _():
                accq[:tplane, :] += jnp.dot(
                    normy[:, cols(jj)], wc[:, :qw], preferred_element_type=jnp.float32
                )

    m_own = x * NCORE + c
    early_enc = rdma(yin.at[blk(m_own)], yout.at[blk(m_own)], e_s, e_r, forward)
    early_dec = rdma(xin, xout, e_s, e_r, forward)

    @pl.when(enc)
    def _():
        early_enc.start()

    @pl.when(dec)
    def _():
        early_dec.start()

    kv_rows = pl.ds(pl.multiple_of(c * plane, plane), plane)
    kv[kv_rows, :] = acckv[...].astype(jnp.bfloat16)
    kv_copy = rdma(kv.at[kv_rows], kv.at[kv_rows], kv_s, kv_r, partner)
    kv_copy.start()
    kv_copy.wait_recv()

    keys = NCORE * plane
    length = len_ref[0]
    n = lax.broadcasted_iota(jnp.int32, (1, keys), 1)
    p_of = (n >= plane).astype(jnp.int32)
    r_of = n - p_of * plane
    position = (r_of // own) * (NCORE * own) + p_of * own + (r_of & (own - 1))
    valid = position < length

    def attention(mq):
        lane = lax.broadcasted_iota(jnp.int32, (mq, lanes), 1)
        for p in range(NCORE):
            qp = accq[:mq, p * lanes : (p + 1) * lanes].astype(jnp.bfloat16)
            kp = kv[:, p * lanes : (p + 1) * lanes]
            vp = kv[:, qw + p * lanes : qw + (p + 1) * lanes]
            outs = []
            for h in range(lanes // HEAD_DIM):
                mine = (lane >= h * HEAD_DIM) & (lane < (h + 1) * HEAD_DIM)
                qh = jnp.where(mine, qp, jnp.zeros_like(qp))
                sc = lax.dot_general(
                    qh, kp, (((1,), (1,)), ((), ())), preferred_element_type=jnp.float32
                )
                sc = jnp.where(valid, sc * 0.125, -1000000000.0)
                ex = jnp.exp(sc - jnp.max(sc, axis=-1, keepdims=True))
                soft = (ex / jnp.sum(ex, axis=-1, keepdims=True)).astype(jnp.bfloat16)
                outs.append(jnp.dot(soft, vp, preferred_element_type=jnp.float32))
            both = outs[0]
            for h in range(1, len(outs)):
                both = jnp.where(lane >= h * HEAD_DIM, outs[h], both)
            ctx[:mq, p * lanes : (p + 1) * lanes] = both.astype(jnp.bfloat16)

    zr = (zu, zd, zh)

    def project(mq, j):
        total = None
        for p in range(NCORE):
            term = lax.dot_general(
                ctx[:mq, p * lanes : (p + 1) * lanes],
                wout[p, cols(j), :],
                (((1,), (1,)), ((), ())),
                preferred_element_type=jnp.float32,
            )
            term = term.astype(jnp.bfloat16).astype(jnp.float32)
            total = term if total is None else total + term
        terms[:mq, cols(j)] = total.astype(jnp.bfloat16)

    def reduction(tblk):
        def c1_copy(r, d, j):
            return rdma(
                terms.at[tblk(x2, r), half(j, d)], r1.at[r, :, half(j, d)], rs_s, c1.at[r, d, j], xdev[d]
            )

        def c2_copy(r, d, j):
            return rdma(
                terms.at[tblk(xnb[d], r), cols(j)], r2.at[r, d, :, cols(j)], rs_s, c2.at[r, d, j], xdev[d]
            )

        def first(r, j):
            for d in range(2):
                c1_copy(r, d, j).start()

        def second(r, j):
            for d in range(2):
                c1_copy(r, d, j).wait_recv()
                at = (tblk(xnb[d], r), half(j, d))
                terms[at] = (
                    terms[at].astype(jnp.float32) + r1[r, :, half(j, d)].astype(jnp.float32)
                ).astype(jnp.bfloat16)
                c2_copy(r, d, j).start()

        def third(r, j):
            for d in range(2):
                c2_copy(r, d, j).wait_recv()
            return (
                terms[tblk(x, r), cols(j)].astype(jnp.float32)
                + r2[r, 0, :, cols(j)].astype(jnp.float32)
                + r2[r, 1, :, cols(j)].astype(jnp.float32)
            ).astype(jnp.bfloat16)

        return first, second, third

    def z_copy(src, u, j, slot):
        return rdma(src, part.at[slot, :, cols(j)], rs_s, c3.at[u, j], zdev[u])

    @pl.when(enc)
    def _():
        attention(plane)
        ld_w[3].wait()
        push_w[3].wait_recv()
        first, second, third = reduction(lambda px, r: blk(px * NZ + zr[r]))

        @pl.loop(0, CHUNKS + 2)
        def _(j):
            @pl.when(j < CHUNKS)
            def _():
                project(plane, j)
                for r in range(2):
                    first(r, j)

            @pl.when((j >= 1) & (j < CHUNKS + 1))
            def _():
                for r in range(2):
                    second(r, j - 1)

            @pl.when(j >= 2)
            def _():
                for u in range(2):
                    zs[u, :, cols(j - 2)] = third(u, j - 2)
                    z_copy(zs.at[u, :, cols(j - 2)], u, j - 2, zh).start()

        @pl.loop(0, CHUNKS)
        def _(j):
            first(2, j)

        @pl.loop(0, CHUNKS)
        def _(j):
            second(2, j)

        @pl.loop(0, CHUNKS)
        def _(j):
            part[zh, :, cols(j)] = third(2, j)

    @pl.when(dec)
    def _():
        attention(tplane)
        ld_w[3].wait()
        push_w[3].wait_recv()
        first, second, third = reduction(lambda px, r: blk(px))

        @pl.loop(0, CHUNKS + 2)
        def _(j):
            @pl.when(j < CHUNKS)
            def _():
                project(tplane, j)
                first(2, j)

            @pl.when((j >= 1) & (j < CHUNKS + 1))
            def _():
                second(2, j - 1)

            @pl.when(j >= 2)
            def _():
                part[zh, :, cols(j - 2)] = third(2, j - 2)
                for u in range(2):
                    z_copy(part.at[zh, :, cols(j - 2)], u, j - 2, zh).start()

    def yx_copy(d, j, m):
        ref = yout.at[blk(m), cols(j)]
        return rdma(ref, ref, y_s, yx.at[d, j], xdev[d])

    def yf_copy(d, j, m):
        ref = yout.at[blk(m), half(j, d)]
        return rdma(ref, ref, y_s, yf.at[d, j], xdev[d])

    def yp_copy(i, j, m):
        ref = yout.at[blk(m), cols(j)]
        return rdma(ref, ref, y_s, yp.at[i, j], partner)

    def late_recv(j):
        rdma(fin.at[:, cols(j)], fin.at[:, cols(j)], l_s, l_r.at[j], forward).wait_recv()

    def spread(arrived):
        @pl.loop(0, CHUNKS)
        def _(j):
            arrived(j)
            for d in range(2):
                yx_copy(d, j, m_own).start()
            yp_copy(0, j, m_own).start()

        @pl.loop(0, CHUNKS)
        def _(j):
            for d, origin in ((0, xl), (1, xr)):
                m = origin * NCORE + c
                yx_copy(d, j, m).wait_recv()
                yf_copy(d, j, m).start()
                yp_copy(1 + d, j, m).start()

        @pl.loop(0, CHUNKS)
        def _(j):
            m = x2 * NCORE + c
            for d in range(2):
                yf_copy(d, j, m).wait_recv()
            yp_copy(3, j, m).start()

    @pl.when(src_enc)
    def _():
        early_dec.wait_recv()
        spread(lambda j: None)

    def late_copy(j, dst):
        return rdma(fin.at[:, cols(j)], dst, l_s, l_r.at[j], forward)

    @pl.loop(0, CHUNKS)
    def _(j):
        for u in range(2):
            z_copy(part.at[zfrom[u], :, cols(j)], u, j, zfrom[u]).wait_recv()
        delta = (
            part[0, :, cols(j)].astype(jnp.float32)
            + part[1, :, cols(j)].astype(jnp.float32)
            + part[2, :, cols(j)].astype(jnp.float32)
        )

        @pl.when(enc)
        def _():
            fin[:, cols(j)] = (xin[:, cols(j)].astype(jnp.float32) + delta).astype(jnp.bfloat16)
            late_copy(j, xout.at[:, cols(j)]).start()

        @pl.when(dec)
        def _():
            fin[:, cols(j)] = (yin[blk(m_own), cols(j)].astype(jnp.float32) + delta).astype(
                jnp.bfloat16
            )
            late_copy(j, yout.at[blk(m_own), cols(j)]).start()

    @pl.when(src_dec)
    def _():
        spread(late_recv)
        early_dec.wait_recv()

    @pl.when(src_enc)
    def _():
        @pl.loop(0, CHUNKS)
        def _(j):
            late_recv(j)

    @pl.loop(0, CHUNKS)
    def _(j):
        for i, px in enumerate((x, xl, xr, x2)):
            yp_copy(i, j, px * NCORE + 1 - c).wait_recv()

    def drain(ref, sem):
        pltpu.make_async_copy(ref, ref, sem).wait()

    drain(wqkv.at[:, : 4 * lanes], w_s)
    drain(rows.at[: 11 * own], ag_s)
    drain(kv.at[:plane], kv_s)
    drain(xin, e_s)
    drain(fin, l_s)
    drain(yout.at[: 7 * own], y_s)

    @pl.when(enc)
    def _():
        drain(terms.at[: 11 * own], rs_s)

    @pl.when(dec)
    def _():
        drain(terms.at[: 5 * own], rs_s)


def local(sections, source_rows, target_rows, attn_weights, gains, lengths):
    weights = attn_weights[0]
    own, width = source_rows.shape
    targets = target_rows.shape[0]
    lanes = weights.shape[2]
    plane = NX * NZ * own
    tplane = NX * own
    bf, f32 = jnp.bfloat16, jnp.float32
    vmem = pltpu.VMEM
    dma = pltpu.SemaphoreType.DMA
    return pl.pallas_call(
        functools.partial(kernel, sections),
        out_shape=(
            jax.ShapeDtypeStruct((own, width), bf),
            jax.ShapeDtypeStruct((targets, width), bf),
        ),
        in_specs=[pl.BlockSpec(memory_space=pl.ANY)] * 4 + [pl.BlockSpec(memory_space=pltpu.SMEM)],
        out_specs=(pl.BlockSpec(memory_space=vmem), pl.BlockSpec(memory_space=vmem)),
        scratch_shapes=[
            vmem((own, width), bf),
            vmem((targets, width), bf),
            vmem((1, width), f32),
            vmem((width, 3 * NCORE * lanes), bf),
            vmem((NCORE, width, lanes), bf),
            vmem((plane, width), bf),
            vmem((tplane, width), bf),
            vmem((plane, NCORE * lanes), f32),
            vmem((plane, 2 * NCORE * lanes), f32),
            vmem((NCORE * plane, 2 * NCORE * lanes), bf),
            vmem((plane, NCORE * lanes), bf),
            vmem((plane, width), bf),
            vmem((3, own, width), bf),
            vmem((3, 2, own, width), bf),
            vmem((2, own, width), bf),
            vmem((NZ, own, width), bf),
            vmem((own, width), bf),
            dma((7,)),
            dma(()),
            dma((4,)),
            dma(()),
            dma((2, CHUNKS)),
            dma((3, 2, CHUNKS)),
            dma((3, 2, CHUNKS)),
            dma(()),
            dma(()),
            dma(()),
            dma(()),
            dma(()),
            dma((3, 2, CHUNKS)),
            dma((3, 2, CHUNKS)),
            dma((2, CHUNKS)),
            dma(()),
            dma((CHUNKS,)),
            dma(()),
            dma((2, CHUNKS)),
            dma((2, CHUNKS)),
            dma((4, CHUNKS)),
        ],
        compiler_params=pltpu.CompilerParams(
            collective_id=0, has_side_effects=True, vmem_limit_bytes=56 * 1024 * 1024
        ),
        name="tick",
    )(source_rows, target_rows, weights, gains, lengths)


def solution(mesh):
    in_specs = (
        P(("section", "fsdp"), None),
        P("section", None),
        P("section", None, None, "fsdp"),
        P("section", None),
        P("section"),
    )
    out_specs = (P(("section", "fsdp"), None), P("section", None))
    body = functools.partial(local, mesh.shape["section"])
    return jax.shard_map(body, mesh=mesh, in_specs=in_specs, out_specs=out_specs, check_vma=False)
```

time: 378 us -> 94.2 us (0.25)
  the two profiles are of different devices: /device:TPU:1 before, /device:TPU:10 now
where the time goes in v1:
time: 94.2 us; the launch traced here: 94 us
  Pallas kernels  88.9 us (94%)
  local copies, waits for them, and re-layouts  3.85 us (4%)
  between operations  1.29 us (1%)
    pallas_call x1, Pallas kernels, local(): pl.pallas_call(functools.partial(kernel, sections), out_shape=(jax.ShapeD...  88.9 us
    unnamed x2, local copies, waits for them, and re-layouts  3.85 us

profile of v1, /device:TPU:10, one launch (start us, length us, event | category | flops | bytes accessed | tf_op | source)
XLA Modules:
  0.0 94.0 jit_solution(11192871369371528060)
XLA Ops:
  1.3 88.9 %tick.1 = (bf16[16,4096]{1,0:T(8,128)(2,1)}, bf16[128,4096]{1,0:T(8,128)(2,1)}) custom-call(bf16[16,4096]{1,0:T(8,128)(2,1)} %x_hbm.1, bf16[128,4096]{1,0:T(8,128)(2,1)} %y_hbm.1, bf16[4,4096,128]{2,1,0:T(8,128)(2,1)} %bitcast.1, f32[1,4096]{1,0:T(1,128)} %g_hbm.1, s32[1]{0:T(128)S(6)} %copy.9.len_ref), custom_call_target="tpu_custom_call" | custom-call | tf_op jit(solution)/shard_map/tick/pallas_call | solution.py:511
  90.2 1.6 %copy.10 = bf16[16,4096]{1,0:T(8,128)(2,1)} copy(bf16[16,4096]{1,0:T(8,128)(2,1)} %get-tuple-element.4) | data formatting | bytes 262144
  91.7 2.3 %copy.11 = bf16[128,4096]{1,0:T(8,128)(2,1)} copy(bf16[128,4096]{1,0:T(8,128)(2,1)} %get-tuple-element.5) | data formatting | bytes 2097152

commit v2 on v1

--- a/solution.py
+++ b/solution.py
@@ -1,3 +1,4 @@
+import contextlib
 import functools
 
 import jax
@@ -12,7 +13,14 @@
 NZ = 3
 NCORE = 2
 CHUNKS = 4
+GATHER_LAG = 4
+REDUCE_LAG = 4
+SPREAD_LAG = 4
 MESH = pl.DeviceIdType.MESH
+
+
+def scope(name):
+    return contextlib.nullcontext()
 
 
 def kernel(
@@ -21,12 +29,13 @@
     y_hbm,
     w_hbm,
     g_hbm,
-    len_ref,
+    len_hbm,
     xout,
     yout,
     xin,
     yin,
     gain,
+    len_ref,
     wqkv,
     wout,
     rows,
@@ -113,6 +122,8 @@
     ld_x.start()
     ld_g.start()
     ld_y.start()
+    ld_n = pltpu.make_async_copy(len_hbm, len_ref, ld.at[7])
+    ld_n.start()
 
     barrier = pltpu.get_barrier_semaphore()
     for dev in (partner, right, left, up, down, forward, backward):
@@ -128,8 +139,9 @@
         copy.start()
 
     k_own = x * NZ + zh
-    ld_x.wait()
-    ld_g.wait()
+    with scope("ld"):
+        ld_x.wait()
+        ld_g.wait()
 
     def normed(block):
         wide = block.astype(jnp.float32)
@@ -144,7 +156,8 @@
     def _():
         rows[blk(k_own), :] = xin[...]
 
-    pl.semaphore_wait(barrier, 7)
+    with scope("barrier"):
+        pl.semaphore_wait(barrier, 7)
 
     zdev = (up, down)
     zb = (zh, zd, zu)
@@ -177,9 +190,11 @@
 
     @pl.when(dec)
     def _():
-        @pl.loop(0, NX)
-        def _(i):
-            normy[blk(i), :] = normed(yin[blk(i * NCORE + c), :])
+        with scope("normy"):
+
+            @pl.loop(0, NX)
+            def _(i):
+                normy[blk(i), :] = normed(yin[blk(i * NCORE + c), :])
 
     def relay(b, j):
         for d, origin in ((0, xl), (1, xr)):
@@ -189,36 +204,44 @@
 
     @pl.loop(0, CHUNKS)
     def _(j):
-        relay(0, j)
+        with scope("relay0"):
+            relay(0, j)
 
     accq[...] = jnp.zeros_like(accq)
     acckv[...] = jnp.zeros_like(acckv)
     qw = NCORE * lanes
 
-    @pl.loop(0, CHUNKS + 1)
+    @pl.loop(0, CHUNKS + 2 * GATHER_LAG)
     def _(j):
         @pl.when(j < CHUNKS)
         def _():
             for u in range(2):
                 k = x * NZ + zfrom[u]
-                az_copy(u, j, k).wait_recv()
+                with scope("az_wait"):
+                    az_copy(u, j, k).wait_recv()
                 for d in range(2):
                     ax_copy(1 + u, d, j, k).start()
-            for b in (1, 2):
-                relay(b, j)
+
+        @pl.when((j >= GATHER_LAG) & (j < CHUNKS + GATHER_LAG))
+        def _():
+            with scope("relay12"):
+                for b in (1, 2):
+                    relay(b, j - GATHER_LAG)
 
         @pl.when(j == 0)
         def _():
-            for i in range(3):
-                ld_w[i].wait()
-                push_w[i].wait_recv()
-
-        @pl.when(j > 0)
+            with scope("w_wait"):
+                for i in range(3):
+                    ld_w[i].wait()
+                    push_w[i].wait_recv()
+
+        @pl.when(j >= 2 * GATHER_LAG)
         def _():
-            jj = j - 1
-            for b in range(3):
-                for d in range(2):
-                    af_copy(b, d, jj, x2 * NZ + zb[b]).wait_recv()
+            jj = j - 2 * GATHER_LAG
+            with scope("af_wait"):
+                for b in range(3):
+                    for d in range(2):
+                        af_copy(b, d, jj, x2 * NZ + zb[b]).wait_recv()
             wc = wqkv.at[cols(jj), :]
             acckv[...] += jnp.dot(rows[:, cols(jj)], wc[:, qw:], preferred_element_type=jnp.float32)
 
@@ -248,9 +271,11 @@
     kv[kv_rows, :] = acckv[...].astype(jnp.bfloat16)
     kv_copy = rdma(kv.at[kv_rows], kv.at[kv_rows], kv_s, kv_r, partner)
     kv_copy.start()
-    kv_copy.wait_recv()
+    with scope("kv_wait"):
+        kv_copy.wait_recv()
 
     keys = NCORE * plane
+    ld_n.wait()
     length = len_ref[0]
     n = lax.broadcasted_iota(jnp.int32, (1, keys), 1)
     p_of = (n >= plane).astype(jnp.int32)
@@ -335,65 +360,78 @@
 
     @pl.when(enc)
     def _():
-        attention(plane)
+        with scope("attention"):
+            attention(plane)
         ld_w[3].wait()
         push_w[3].wait_recv()
         first, second, third = reduction(lambda px, r: blk(px * NZ + zr[r]))
 
-        @pl.loop(0, CHUNKS + 2)
-        def _(j):
-            @pl.when(j < CHUNKS)
-            def _():
-                project(plane, j)
+        @pl.loop(0, 2 * CHUNKS + 2 * REDUCE_LAG)
+        def _(i):
+            @pl.when(i < CHUNKS)
+            def _():
+                with scope("project"):
+                    project(plane, i)
                 for r in range(2):
-                    first(r, j)
-
-            @pl.when((j >= 1) & (j < CHUNKS + 1))
-            def _():
-                for r in range(2):
-                    second(r, j - 1)
-
-            @pl.when(j >= 2)
-            def _():
+                    first(r, i)
+
+            @pl.when((i >= CHUNKS) & (i < 2 * CHUNKS))
+            def _():
+                first(2, i - CHUNKS)
+
+            @pl.when((i >= REDUCE_LAG) & (i < CHUNKS + REDUCE_LAG))
+            def _():
+                with scope("second"):
+                    for r in range(2):
+                        second(r, i - REDUCE_LAG)
+
+            @pl.when((i >= CHUNKS + REDUCE_LAG) & (i < 2 * CHUNKS + REDUCE_LAG))
+            def _():
+                with scope("second_own"):
+                    second(2, i - CHUNKS - REDUCE_LAG)
+
+            @pl.when((i >= 2 * REDUCE_LAG) & (i < CHUNKS + 2 * REDUCE_LAG))
+            def _():
+                j = i - 2 * REDUCE_LAG
                 for u in range(2):
-                    zs[u, :, cols(j - 2)] = third(u, j - 2)
-                    z_copy(zs.at[u, :, cols(j - 2)], u, j - 2, zh).start()
-
-        @pl.loop(0, CHUNKS)
-        def _(j):
-            first(2, j)
-
-        @pl.loop(0, CHUNKS)
-        def _(j):
-            second(2, j)
-
-        @pl.loop(0, CHUNKS)
-        def _(j):
-            part[zh, :, cols(j)] = third(2, j)
+                    with scope("third"):
+                        zs[u, :, cols(j)] = third(u, j)
+                    z_copy(zs.at[u, :, cols(j)], u, j, zh).start()
+
+            @pl.when(i >= CHUNKS + 2 * REDUCE_LAG)
+            def _():
+                j = i - CHUNKS - 2 * REDUCE_LAG
+                with scope("third_own"):
+                    part[zh, :, cols(j)] = third(2, j)
 
     @pl.when(dec)
     def _():
-        attention(tplane)
+        with scope("attention"):
+            attention(tplane)
         ld_w[3].wait()
         push_w[3].wait_recv()
         first, second, third = reduction(lambda px, r: blk(px))
 
-        @pl.loop(0, CHUNKS + 2)
-        def _(j):
-            @pl.when(j < CHUNKS)
-            def _():
-                project(tplane, j)
-                first(2, j)
-
-            @pl.when((j >= 1) & (j < CHUNKS + 1))
-            def _():
-                second(2, j - 1)
-
-            @pl.when(j >= 2)
-            def _():
-                part[zh, :, cols(j - 2)] = third(2, j - 2)
+        @pl.loop(0, CHUNKS + 2 * REDUCE_LAG)
+        def _(i):
+            @pl.when(i < CHUNKS)
+            def _():
+                with scope("project"):
+                    project(tplane, i)
+                first(2, i)
+
+            @pl.when((i >= REDUCE_LAG) & (i < CHUNKS + REDUCE_LAG))
+            def _():
+                with scope("second"):
+                    second(2, i - REDUCE_LAG)
+
+            @pl.when(i >= 2 * REDUCE_LAG)
+            def _():
+                j = i - 2 * REDUCE_LAG
+                with scope("third"):
+                    part[zh, :, cols(j)] = third(2, j)
                 for u in range(2):
-                    z_copy(part.at[zh, :, cols(j - 2)], u, j - 2, zh).start()
+                    z_copy(part.at[zh, :, cols(j)], u, j, zh).start()
 
     def yx_copy(d, j, m):
         ref = yout.at[blk(m), cols(j)]
@@ -410,41 +448,43 @@
     def late_recv(j):
         rdma(fin.at[:, cols(j)], fin.at[:, cols(j)], l_s, l_r.at[j], forward).wait_recv()
 
-    def spread(arrived):
+    def spread_first(j):
+        for d in range(2):
+            yx_copy(d, j, m_own).start()
+        yp_copy(0, j, m_own).start()
+
+    def spread_second(j):
+        for d, origin in ((0, xl), (1, xr)):
+            m = origin * NCORE + c
+            with scope("yx_wait"):
+                yx_copy(d, j, m).wait_recv()
+            yf_copy(d, j, m).start()
+            yp_copy(1 + d, j, m).start()
+
+    def spread_third(j):
+        m = x2 * NCORE + c
+        with scope("yf_wait"):
+            for d in range(2):
+                yf_copy(d, j, m).wait_recv()
+        yp_copy(3, j, m).start()
+
+    @pl.when(src_enc)
+    def _():
+        with scope("early_wait"):
+            early_dec.wait_recv()
+
         @pl.loop(0, CHUNKS)
         def _(j):
-            arrived(j)
-            for d in range(2):
-                yx_copy(d, j, m_own).start()
-            yp_copy(0, j, m_own).start()
-
-        @pl.loop(0, CHUNKS)
-        def _(j):
-            for d, origin in ((0, xl), (1, xr)):
-                m = origin * NCORE + c
-                yx_copy(d, j, m).wait_recv()
-                yf_copy(d, j, m).start()
-                yp_copy(1 + d, j, m).start()
-
-        @pl.loop(0, CHUNKS)
-        def _(j):
-            m = x2 * NCORE + c
-            for d in range(2):
-                yf_copy(d, j, m).wait_recv()
-            yp_copy(3, j, m).start()
-
-    @pl.when(src_enc)
-    def _():
-        early_dec.wait_recv()
-        spread(lambda j: None)
+            spread_first(j)
 
     def late_copy(j, dst):
         return rdma(fin.at[:, cols(j)], dst, l_s, l_r.at[j], forward)
 
     @pl.loop(0, CHUNKS)
     def _(j):
-        for u in range(2):
-            z_copy(part.at[zfrom[u], :, cols(j)], u, j, zfrom[u]).wait_recv()
+        with scope("z_wait"):
+            for u in range(2):
+                z_copy(part.at[zfrom[u], :, cols(j)], u, j, zfrom[u]).wait_recv()
         delta = (
             part[0, :, cols(j)].astype(jnp.float32)
             + part[1, :, cols(j)].astype(jnp.float32)
@@ -465,24 +505,50 @@
 
     @pl.when(src_dec)
     def _():
-        spread(late_recv)
+        @pl.loop(0, CHUNKS + 2 * SPREAD_LAG)
+        def _(j):
+            @pl.when(j < CHUNKS)
+            def _():
+                with scope("late_wait"):
+                    late_recv(j)
+                spread_first(j)
+
+            @pl.when((j >= SPREAD_LAG) & (j < CHUNKS + SPREAD_LAG))
+            def _():
+                spread_second(j - SPREAD_LAG)
+
+            @pl.when(j >= 2 * SPREAD_LAG)
+            def _():
+                spread_third(j - 2 * SPREAD_LAG)
+
         early_dec.wait_recv()
 
     @pl.when(src_enc)
     def _():
         @pl.loop(0, CHUNKS)
         def _(j):
-            late_recv(j)
+            spread_second(j)
+
+        @pl.loop(0, CHUNKS)
+        def _(j):
+            spread_third(j)
+
+        @pl.loop(0, CHUNKS)
+        def _(j):
+            with scope("late_wait"):
+                late_recv(j)
 
     @pl.loop(0, CHUNKS)
     def _(j):
-        for i, px in enumerate((x, xl, xr, x2)):
-            yp_copy(i, j, px * NCORE + 1 - c).wait_recv()
+        with scope("yp_wait"):
+            for i, px in enumerate((x, xl, xr, x2)):
+                yp_copy(i, j, px * NCORE + 1 - c).wait_recv()
 
     def drain(ref, sem):
         pltpu.make_async_copy(ref, ref, sem).wait()
 
-    drain(wqkv.at[:, : 4 * lanes], w_s)
+    with scope("drain0"):
+        drain(wqkv.at[:, : 4 * lanes], w_s)
     drain(rows.at[: 11 * own], ag_s)
     drain(kv.at[:plane], kv_s)
     drain(xin, e_s)
@@ -496,6 +562,17 @@
     @pl.when(dec)
     def _():
         drain(terms.at[: 5 * own], rs_s)
+
+
+def write_out(x_ref, y_ref, x_out, y_out, sem):
+    copies = [
+        pltpu.make_async_copy(x_ref, x_out, sem.at[0]),
+        pltpu.make_async_copy(y_ref, y_out, sem.at[1]),
+    ]
+    for copy in copies:
+        copy.start()
+    for copy in copies:
+        copy.wait()
 
 
 def local(sections, source_rows, target_rows, attn_weights, gains, lengths):
@@ -508,18 +585,16 @@
     bf, f32 = jnp.bfloat16, jnp.float32
     vmem = pltpu.VMEM
     dma = pltpu.SemaphoreType.DMA
-    return pl.pallas_call(
+    results = pl.pallas_call(
         functools.partial(kernel, sections),
-        out_shape=(
-            jax.ShapeDtypeStruct((own, width), bf),
-            jax.ShapeDtypeStruct((targets, width), bf),
-        ),
-        in_specs=[pl.BlockSpec(memory_space=pl.ANY)] * 4 + [pl.BlockSpec(memory_space=pltpu.SMEM)],
+        out_shape=(vmem((own, width), bf), vmem((targets, width), bf)),
+        in_specs=[pl.BlockSpec(memory_space=pltpu.HBM)] * 5,
         out_specs=(pl.BlockSpec(memory_space=vmem), pl.BlockSpec(memory_space=vmem)),
         scratch_shapes=[
             vmem((own, width), bf),
             vmem((targets, width), bf),
             vmem((1, width), f32),
+            pltpu.SMEM((1,), jnp.int32),
             vmem((width, 3 * NCORE * lanes), bf),
             vmem((NCORE, width, lanes), bf),
             vmem((plane, width), bf),
@@ -534,7 +609,7 @@
             vmem((2, own, width), bf),
             vmem((NZ, own, width), bf),
             vmem((own, width), bf),
-            dma((7,)),
+            dma((8,)),
             dma(()),
             dma((4,)),
             dma(()),
@@ -561,6 +636,18 @@
         ),
         name="tick",
     )(source_rows, target_rows, weights, gains, lengths)
+    return pl.pallas_call(
+        write_out,
+        out_shape=(
+            jax.ShapeDtypeStruct((own, width), bf),
+            jax.ShapeDtypeStruct((targets, width), bf),
+        ),
+        in_specs=[pl.BlockSpec(memory_space=vmem)] * 2,
+        out_specs=(pl.BlockSpec(memory_space=pl.ANY), pl.BlockSpec(memory_space=pl.ANY)),
+        scratch_shapes=[dma((2,))],
+        compiler_params=pltpu.CompilerParams(vmem_limit_bytes=1024 * 1024),
+        name="write_out",
+    )(*results)
 
 
 def solution(mesh):

time: 94.2 us -> 79.1 us (0.84)
  the two profiles are of different devices: /device:TPU:10 before, /device:TPU:1 now
where the time goes in v2:
time: 79.1 us; the launch traced here: 78.7 us
  Pallas kernels  77.4 us (98%)
  between operations  1.29 us (2%)
    pallas_call x1, Pallas kernels, local(): pl.pallas_call(functools.partial(kernel, sections), out_shape=(vmem((own,...  76.4 us

profile of v2, /device:TPU:1, one launch (start us, length us, event | category | flops | bytes accessed | tf_op | source)
XLA Modules:
  0.0 78.7 jit_solution(3839603921427531034)
XLA Ops:
  1.3 76.4 %tick.1 = (bf16[16,4096]{1,0:T(8,128)(2,1)S(1)}, bf16[128,4096]{1,0:T(8,128)(2,1)S(1)}) custom-call(bf16[16,4096]{1,0:T(8,128)(2,1)} %x_hbm.1, bf16[128,4096]{1,0:T(8,128)(2,1)} %y_hbm.1, bf16[4,4096,128]{2,1,0:T(8,128)(2,1)} %bitcast.1, f32[1,4096]{1,0:T(1,128)} %g_hbm.1, s32[1]{0:T(128)S(6)} %copy.7.len_hbm), custom_call_target="tpu_custom_call" | custom-call | tf_op jit(solution)/shard_map/tick/pallas_call | solution.py:588
  77.7 1.0 %write_out.1 = (bf16[16,4096]{1,0:T(8,128)(2,1)}, bf16[128,4096]{1,0:T(8,128)(2,1)}) custom-call(bf16[16,4096]{1,0:T(8,128)(2,1)S(1)} %get-tuple-element.4.x_ref, bf16[128,4096]{1,0:T(8,128)(2,1)S(1)} %get-tuple-element.5.y_ref), custom_call_target="tpu_custom_call" | custom-call | tf_op jit(solution)/shard_map/write_out/pallas_call | solution.py:639
